TPU v7x, 32 devices: a whole 2x2x4 slice. The times are simulated.
32 devices in a mesh: gx: 8 (over y, x, core), gy: 4 (over z).
Axes of the slice: x: 2, y: 2, z: 4, core: 2. Of those that a mesh axis runs over, the one named last changes fastest.
Arguments:
- field: float32 [65536, 512], P(('gx', 'gy')), may hold values from -6 to 6
Outputs:
- spectrum: float32 [65536, 512], P('gx', 'gy')
All inputs are finite; a program needn't handle non-finite values.
Results may differ from a plain program's by a relative error of at most 0.00007.
Values sent between devices are 32-bit elements; how exact they have to be, the bound alone decides.
A program may use at most 64 MiB of HBM per device.

v0:
```python
import math
import jax
import jax.numpy as jnp
from jax import lax
from jax.sharding import PartitionSpec as P

P_SIZE = 256
Q = 256
highest = lax.Precision.HIGHEST


def mat_dot(left, right):
    return jnp.dot(left, right, precision=highest, preferred_element_type=jnp.float32)


def finish(spec_real, spec_imag, frequency):
    length = P_SIZE * Q
    phases = math.pi / (2.0 * length) * frequency.astype(jnp.float32)
    factor = math.sqrt(2.0 / length)
    return factor * (
        jnp.cos(phases)[:, :, None] * spec_real + jnp.sin(phases)[:, :, None] * spec_imag
    )


def body(field):
    groups = lax.axis_size("gx")
    position = lax.axis_index("gx")
    length = P_SIZE * Q
    joined = lax.all_to_all(field, "gy", split_axis=1, concat_axis=0, tiled=True)
    row_count = joined.shape[0]
    col_width = joined.shape[1]
    half_rows = P_SIZE // (2 * groups)
    local_q = Q // groups
    local_p = P_SIZE // groups
    paired = joined.reshape(row_count // 2, 2, col_width)
    even_rows = paired[:, 0].reshape(half_rows, Q, col_width)
    odd_rows = jnp.flip(paired[:, 1].reshape(half_rows, Q, col_width), axis=1)
    low_half, high_half = (
        lax.all_to_all(even_rows, "gx", split_axis=1, concat_axis=0, tiled=True),
        lax.all_to_all(odd_rows, "gx", split_axis=1, concat_axis=0, tiled=True),
    )
    freq_first = jnp.arange(P_SIZE, dtype=jnp.int32)
    place_low = jnp.arange(P_SIZE // 2, dtype=jnp.int32)
    place_high = P_SIZE - 1 - place_low
    two_pi = 2.0 * math.pi
    low_phase = (
        two_pi / P_SIZE * (freq_first[:, None] * place_low[None, :] % P_SIZE).astype(jnp.float32)
    )
    high_phase = (
        two_pi / P_SIZE * (freq_first[:, None] * place_high[None, :] % P_SIZE).astype(jnp.float32)
    )
    flat_low = low_half.reshape(P_SIZE // 2, local_q * col_width)
    flat_high = high_half.reshape(P_SIZE // 2, local_q * col_width)
    cos_part = (
        mat_dot(jnp.cos(low_phase), flat_low) + mat_dot(jnp.cos(high_phase), flat_high)
    ).reshape(P_SIZE, local_q, col_width)
    sin_part = (
        mat_dot(jnp.sin(low_phase), flat_low) + mat_dot(jnp.sin(high_phase), flat_high)
    ).reshape(P_SIZE, local_q, col_width)
    part_imag = -sin_part
    second_place = position * local_q + jnp.arange(local_q, dtype=jnp.int32)
    turn_phase = (
        two_pi / length * (freq_first[:, None] * second_place[None, :] % length).astype(jnp.float32)
    )
    turn_cos = jnp.cos(turn_phase)[:, :, None]
    turn_sin = jnp.sin(turn_phase)[:, :, None]
    turned_real = cos_part * turn_cos + part_imag * turn_sin
    turned_imag = part_imag * turn_cos - cos_part * turn_sin
    moved_real, moved_imag = (
        lax.all_to_all(turned_real, "gx", split_axis=0, concat_axis=1, tiled=True),
        lax.all_to_all(turned_imag, "gx", split_axis=0, concat_axis=1, tiled=True),
    )
    second_index = jnp.arange(Q, dtype=jnp.int32)
    row_phase = two_pi / Q * (second_index[:, None] * second_index[None, :] % Q).astype(jnp.float32)
    row_cos = jnp.cos(row_phase)
    row_sin = jnp.sin(row_phase)
    spec_real = jnp.einsum("jb,kbc->jkc", row_cos, moved_real, precision=highest) + jnp.einsum(
        "jb,kbc->jkc", row_sin, moved_imag, precision=highest
    )
    spec_imag = jnp.einsum("jb,kbc->jkc", row_cos, moved_imag, precision=highest) - jnp.einsum(
        "jb,kbc->jkc", row_sin, moved_real, precision=highest
    )
    block_rows = lax.dynamic_slice_in_dim(freq_first, position * local_p, local_p, 0)
    frequency = block_rows[None, :] + P_SIZE * second_index[:, None]
    result = finish(spec_real, spec_imag, frequency)
    arrived = lax.all_to_all(result, "gx", split_axis=0, concat_axis=1, tiled=True)
    return arrived.reshape(local_q * P_SIZE, col_width)


def solution(mesh):
    in_specs = (P(("gx", "gy"), None),)
    out_specs = P("gx", "gy")
    return jax.shard_map(body, mesh=mesh, in_specs=in_specs, out_specs=out_specs, check_vma=False)
```

profile of v0, /device:TPU:0, one launch (start us, length us, event | category | flops | bytes accessed | tf_op | source)
XLA Modules:
  0.0 380.9 jit_solution(13258083812697321297)
XLA Ops:
  0.0 5.3 %copy.15 = f32[2048,512]{0,1:T(8,128)} copy(f32[2048,512]{1,0:T(8,128)} %param.1) | data formatting | bytes 8388608 | tf_op args[0]
  5.3 100.6 %all_to_all.97 = f32[2048,4,128]{0,2,1:T(8,128)} all-to-all(f32[2048,4,128]{0,2,1:T(8,128)} %bitcast.81), channel_id=1, replica_groups=mesh['gx'=8,'gy'=4] {'gy'}, dimensions={1} | all-to-all | bytes 8388608 | tf_op jit(solution)/shard_map/all_to_all | solution.py:29
  105.9 5.3 %copy.16 = f32[4,2048,128]{2,1,0:T(8,128)} copy(f32[4,2048,128]{1,2,0:T(8,128)} %bitcast.79) | data formatting | bytes 8388608 | tf_op jit(solution)/shard_map/all_to_all | solution.py:29
  111.2 7.7 %fusion.96 = (f32[4096,1,128]{2,1,0:T(1,128)}, f32[4096,1,128]{2,1,0:T(1,128)S(1)}) fusion(f32[4096,2,128]{2,1,0:T(2,128)} %bitcast.78), kind=kLoop, calls=%fused_computation.111 | loop fusion | bytes 8388608 | tf_op jit(solution)/shard_map/slice | solution.py:37
  118.9 2.5 copy.17
  121.4 3.8 all-to-all-start.1
  125.2 4.1 %copy.20 = f32[16,256,128]{2,0,1:T(8,128)} copy(f32[16,256,128]{2,1,0:T(8,128)} %bitcast.83) | data formatting | bytes 4194304 | tf_op jit(solution)/shard_map/reshape;squeeze | solution.py:37
  129.3 3.1 rev.4
  132.4 19.4 %all-to-all-done.1 = f32[16,256,128]{2,0,1:T(8,128)S(1)} async-done(((f32[16,256,128]{2,0,1:T(8,128)}), f32[16,256,128]{2,0,1:T(8,128)S(1)}, u32[]{:S(2)}, u32[]{:S(2)}) %all-to-all-start.1) | async-done | bytes 2097184 | tf_op jit(solution)/shard_map/all_to_all | solution.py:39
  151.8 4.9 %all-to-all-start.2 = ((f32[16,256,128]{2,0,1:T(8,128)}), f32[16,256,128]{2,0,1:T(8,128)}, u32[]{:S(2)}, u32[]{:S(2)}) async-start(f32[16,256,128]{2,0,1:T(8,128)} %rev.4), calls=%async_computation.2 | async-start | bytes 4194304 | tf_op jit(solution)/shard_map/all_to_all | solution.py:40
  156.7 0.5 fusion.57
  157.3 0.6 copy.19
  157.9 7.3 %fusion.9 = f32[256,4096]{1,0:T(8,128)} fusion(f32[16,8,32,128]{3,2,1,0:T(8,128)S(1)} %bitcast.73), kind=kOutput, calls=%fused_computation.16 | convolution fusion | flops 1611071488 | bytes 6291456 | tf_op jit(solution)/shard_map/dot_general | solution.py:13
  165.2 7.5 %fusion.7 = f32[256,4096]{1,0:T(8,128)} fusion(f32[16,8,32,128]{3,2,1,0:T(8,128)S(1)} %bitcast.74), kind=kOutput, calls=%fused_computation.14 | convolution fusion | flops 1611071488 | bytes 6291456 | tf_op jit(solution)/shard_map/dot_general | solution.py:13
  172.7 10.6 %all-to-all-done.2 = f32[16,256,128]{2,0,1:T(8,128)} async-done(((f32[16,256,128]{2,0,1:T(8,128)}), f32[16,256,128]{2,0,1:T(8,128)}, u32[]{:S(2)}, u32[]{:S(2)}) %all-to-all-start.2) | async-done | bytes 2097184 | tf_op jit(solution)/shard_map/all_to_all | solution.py:40
  183.3 0.0 copy-start.3
  183.3 2.4 copy.22
  185.7 0.4 copy-done.3
  186.1 4.9 %fusion.3 = f32[32,8,32,128]{3,1,2,0:T(8,128)S(1)} fusion(f32[256,4096]{1,0:T(8,128)S(1)} %copy-done.3, f32[16,8,32,128]{3,2,1,0:T(8,128)S(1)} %bitcast.75, s32[128]{0:T(128)S(1)} %iota_subtract_fusion), kind=kOutput, calls=%fused_computation.10 | convolution fusion | flops 1612120064 | bytes 10486272 | tf_op jit(solution)/shard_map/dot_general | solution.py:13
  191.1 0.0 copy-start.2
  191.1 0.8 copy.31
  191.9 1.4 copy-done.2
  193.3 5.0 %fusion.4 = f32[32,8,32,128]{3,1,2,0:T(8,128)S(1)} fusion(f32[256,4096]{1,0:T(8,128)S(1)} %copy-done.2, f32[16,8,32,128]{3,2,1,0:T(8,128)S(1)} %bitcast.76, s32[128]{0:T(128)S(1)} %iota_subtract_fusion), kind=kOutput, calls=%fused_computation.11 | convolution fusion | flops 1613168640 | bytes 10486272 | tf_op jit(solution)/shard_map/dot_general | solution.py:13
  198.2 1.0 copy.32
  199.2 4.6 %fusion.1 = (f32[256,32,128]{2,1,0:T(8,128)}, f32[256,32,128]{2,1,0:T(8,128)S(1)}) fusion(f32[32,8,32,128]{3,2,1,0:T(8,128)S(1)} %copy.32, f32[32,8,32,128]{3,2,1,0:T(8,128)S(1)} %copy.31, f32[256,32]{1,0:T(8,128)S(1)} %get-tuple-element.12, f32[256,32]{1,0:T(8,128)S(1)} %get-tuple-element.11), kind=kLoop, calls=%fused_computation.5 | loop fusion | flops 6291456 | bytes 16842752 | tf_op jit(solution)/shard_map/add | solution.py:67
  203.8 52.3 %all_to_all.98 = f32[256,32,128]{2,1,0:T(8,128)} all-to-all(f32[256,32,128]{2,1,0:T(8,128)S(1)} %get-tuple-element.6), channel_id=1, replica_groups=mesh['gx'=8,'gy'=4] {'gx'}, dimensions={0} | all-to-all | bytes 8388608 | tf_op jit(solution)/shard_map/all_to_all | solution.py:71
  256.1 4.6 %all-to-all-start.3 = ((f32[256,32,128]{2,1,0:T(8,128)}), f32[256,32,128]{2,1,0:T(8,128)}, u32[]{:S(2)}, u32[]{:S(2)}) async-start(f32[256,32,128]{2,1,0:T(8,128)} %get-tuple-element.5), calls=%async_computation.3 | async-start | bytes 8388608 | tf_op jit(solution)/shard_map/all_to_all | solution.py:70
  260.7 0.1 dynamic_slice.3
  260.8 0.2 fusion.63
  261.0 2.8 copy.24
  263.8 7.1 %fusion.19 = f32[256,32,128]{2,0,1:T(8,128)} fusion(f32[32,256,128]{2,1,0:T(8,128)S(1)} %bitcast.71), kind=kOutput, calls=%fused_computation.29 | convolution fusion | flops 3222142976 | bytes 8388608 | tf_op jit(solution)/shard_map/jb,kbc->jkc/dot_general | solution.py:77
  270.9 7.3 %fusion.21 = f32[256,32,128]{2,0,1:T(8,128)} fusion(f32[32,256,128]{2,1,0:T(8,128)S(1)} %bitcast.72), kind=kOutput, calls=%fused_computation.31 | convolution fusion | flops 3222142976 | bytes 8388608 | tf_op jit(solution)/shard_map/jb,kbc->jkc/dot_general | solution.py:80
  278.2 31.5 %all-to-all-done.3 = f32[256,32,128]{2,1,0:T(8,128)} async-done(((f32[256,32,128]{2,1,0:T(8,128)}), f32[256,32,128]{2,1,0:T(8,128)}, u32[]{:S(2)}, u32[]{:S(2)}) %all-to-all-start.3) | async-done | bytes 4194336 | tf_op jit(solution)/shard_map/all_to_all | solution.py:70
  309.8 2.8 copy.23
  312.6 0.0 copy-start
  312.6 0.0 copy-start.1
  312.6 4.8 %fusion.23 = f32[256,32,128]{2,0,1:T(8,128)S(1)} fusion(f32[32,256,128]{2,1,0:T(8,128)S(1)} %bitcast.69), kind=kOutput, calls=%fused_computation.33 | convolution fusion | flops 3222142976 | bytes 8388608 | tf_op jit(solution)/shard_map/jb,kbc->jkc/dot_general | solution.py:77
  317.4 0.0 copy-done
  317.4 0.0 copy-done.1
  317.4 6.1 %add_multiply_fusion = f32[256,32,128]{2,0,1:T(8,128)S(1)} fusion(f32[256,32,128]{2,0,1:T(8,128)S(1)} %copy-done.1, f32[256,32,128]{2,0,1:T(8,128)S(1)} %fusion.23, f32[256,32,128]{2,0,1:T(8,128)S(1)} %copy-done, f32[32,256,128]{2,1,0:T(8,128)S(1)} %bitcast.70, f32[256,32]{0,1:T(8,128)S(1)} %get-tuple-element.10, f32[256,32]{0,1:T(8,128)S(1)} %get-tuple-element.9), kind=kOutput, calls=%fused_computation.9 | convolution fusion | flops 3228434432 | bytes 21037056 | tf_op jit(solution)/shard_map/jb,kbc->jkc/dot_general | solution.py:80
  323.5 2.7 copy.25
  326.3 51.5 %all_to_all.99 = f32[256,32,128]{2,1,0:T(8,128)S(1)} all-to-all(f32[256,32,128]{2,1,0:T(8,128)S(1)} %copy.25), channel_id=1, replica_groups=mesh['gx'=8,'gy'=4] {'gx'}, dimensions={0} | all-to-all | bytes 8388608 | tf_op jit(solution)/shard_map/all_to_all | solution.py:86
  377.8 2.7 copy.26
  (4 shorter events, 0.0 us)
Async XLA Ops:
  121.4 30.4 %all-to-all-start.1 = ((f32[16,256,128]{2,0,1:T(8,128)}), f32[16,256,128]{2,0,1:T(8,128)S(1)}, u32[]{:S(2)}, u32[]{:S(2)}) async-start(f32[16,256,128]{2,0,1:T(8,128)} %copy.17), calls=%async_computation.1 | async-start | bytes 4194304 | tf_op jit(solution)/shard_map/all_to_all | solution.py:39
  151.8 31.5 %all-to-all-start.2 = ((f32[16,256,128]{2,0,1:T(8,128)}), f32[16,256,128]{2,0,1:T(8,128)}, u32[]{:S(2)}, u32[]{:S(2)}) async-start(f32[16,256,128]{2,0,1:T(8,128)} %rev.4), calls=%async_computation.2 | async-start | bytes 4194304 | tf_op jit(solution)/shard_map/all_to_all | solution.py:40
  183.3 2.8 copy-start.3
  191.1 2.2 copy-start.2
  256.1 53.7 %all-to-all-start.3 = ((f32[256,32,128]{2,1,0:T(8,128)}), f32[256,32,128]{2,1,0:T(8,128)}, u32[]{:S(2)}, u32[]{:S(2)}) async-start(f32[256,32,128]{2,1,0:T(8,128)} %get-tuple-element.5), calls=%async_computation.3 | async-start | bytes 8388608 | tf_op jit(solution)/shard_map/all_to_all | solution.py:70
  312.6 4.8 %copy-start = (f32[256,32,128]{2,0,1:T(8,128)S(1)}, f32[256,32,128]{2,0,1:T(8,128)}, u32[]{:S(2)}) copy-start(f32[256,32,128]{2,0,1:T(8,128)} %fusion.19) | copy-start | bytes 12582916
  312.6 4.8 %copy-start.1 = (f32[256,32,128]{2,0,1:T(8,128)S(1)}, f32[256,32,128]{2,0,1:T(8,128)}, u32[]{:S(2)}) copy-start(f32[256,32,128]{2,0,1:T(8,128)} %fusion.21) | copy-start | bytes 12582916
where the time goes:
time: 386 us; the launch traced here: 381 us
  blocking collectives  204 us (53%)
  waiting for transfers between devices  61.6 us (16%)
  matrix products  50 us (13%)
  local copies, waits for them, and re-layouts  45.8 us (12%)
  starting transfers between devices  13.2 us (3%)
  other arithmetic  5.36 us (1%)
    all_to_all x1, blocking collectives, body(): lax.all_to_all(field, 'gy', split_axis=1, concat_axis=0, tiled=True)  101 us
    all_to_all x1, blocking collectives, body(): lax.all_to_all(turned_imag, 'gx', split_axis=0, concat_axis=1, tiled=True)  52.3 us
    all_to_all x1, blocking collectives, body(): lax.all_to_all(result, 'gx', split_axis=0, concat_axis=1, tiled=True)  51.5 us
    all_to_all x1, waiting for transfers between devices, body(): lax.all_to_all(turned_real, 'gx', split_axis=0, concat_axis=1, tiled=True)  31.5 us
    dot_general x4, matrix products, mat_dot(): jnp.dot(left, right, precision=highest, preferred_element_type=jnp.float32)  24.7 us
    all_to_all x1, waiting for transfers between devices, body(): lax.all_to_all(even_rows, 'gx', split_axis=1, concat_axis=0, tiled=True)  19.4 us
    all_to_all x1, waiting for transfers between devices, body(): lax.all_to_all(odd_rows, 'gx', split_axis=1, concat_axis=0, tiled=True)  10.6 us
    unnamed x11, local copies, waits for them, and re-layouts  8.93 us
  transfers between devices with their start and end apart: 3, of which 3 were waited for; matrix products, arithmetic and copies ran while one was open for 11% of the time, Pallas kernels for 0%

commit v1 on v0

--- a/solution.py
+++ b/solution.py
@@ -7,6 +7,22 @@
 P_SIZE = 256
 Q = 256
 highest = lax.Precision.HIGHEST
+
+
+def pairwise_exchange(array, axis, split, join):
+    ways, here = (lax.axis_size(axis), lax.axis_index(axis))
+    width = array.shape[split] // ways
+    dims = list(array.shape)
+    dims[split] = width
+    height = dims[join]
+    dims[join] = height * ways
+    full = jnp.zeros(dims, array.dtype)
+    for mask in range(ways):
+        part = lax.dynamic_slice_in_dim(array, (here ^ mask) * width, width, axis=split)
+        if mask:
+            part = lax.ppermute(part, axis, [(d, d ^ mask) for d in range(ways)])
+        full = lax.dynamic_update_slice_in_dim(full, part, (here ^ mask) * height, axis=join)
+    return full
 
 
 def mat_dot(left, right):
@@ -36,7 +52,7 @@
     even_rows = paired[:, 0].reshape(half_rows, Q, col_width)
     odd_rows = jnp.flip(paired[:, 1].reshape(half_rows, Q, col_width), axis=1)
     low_half, high_half = (
-        lax.all_to_all(even_rows, "gx", split_axis=1, concat_axis=0, tiled=True),
+        pairwise_exchange(even_rows, "gx", 1, 0),
         lax.all_to_all(odd_rows, "gx", split_axis=1, concat_axis=0, tiled=True),
     )
     freq_first = jnp.arange(P_SIZE, dtype=jnp.int32)

time: 386 us -> 384 us (level)
  waiting for transfers between devices: 61.6 us -> 66.5 us
  matrix products: 50 us -> 45.2 us
  local copies, waits for them, and re-layouts: 45.8 us -> 41.7 us
    ppermute x0 -> x7, waiting for transfers between devices: none -> 34.9 us  [pairwise_exchange(): part = lax.ppermute(part, axis, [(d, d ^ mask) for d in range(ways)])]
    all_to_all x1 -> x0, waiting for transfers between devices: 19.4 us -> none  [body(): lax.all_to_all(even_rows, 'gx', split_axis=1, concat_axis=0, tiled=True)]
    all_to_all x1, waiting for transfers between devices: 10.6 us -> 0.01 us  [body(): lax.all_to_all(odd_rows, 'gx', split_axis=1, concat_axis=0, tiled=True)]
    ppermute x0 -> x7, starting transfers between devices: none -> 6.49 us  [pairwise_exchange(): part = lax.ppermute(part, axis, [(d, d ^ mask) for d in range(ways)])]
    dot_general x4, matrix products: 24.7 us -> 19.9 us  [mat_dot(): jnp.dot(left, right, precision=highest, preferred_element_type=jnp.float32)]
    unnamed x11 -> x7, local copies, waits for them, and re-layouts: 8.93 us -> 6.86 us
  transfers between devices with their start and end apart: 3 -> 9, of which waited for: 3 -> 5; matrix products, arithmetic and copies ran while one was open for 11% -> 6% of each run, Pallas kernels for 0% -> 0%
where the time goes in v1:
time: 384 us; the launch traced here: 380 us
  blocking collectives  204 us (53%)
  waiting for transfers between devices  66.5 us (17%)
  matrix products  45.2 us (12%)
  local copies, waits for them, and re-layouts  41.7 us (11%)
  starting transfers between devices  15.9 us (4%)
  other arithmetic  5.57 us (1%)
    all_to_all x1, blocking collectives, body(): lax.all_to_all(field, 'gy', split_axis=1, concat_axis=0, tiled=True)  101 us
    all_to_all x1, blocking collectives, body(): lax.all_to_all(turned_imag, 'gx', split_axis=0, concat_axis=1, tiled=True)  52.3 us
    all_to_all x1, blocking collectives, body(): lax.all_to_all(result, 'gx', split_axis=0, concat_axis=1, tiled=True)  51.5 us
    ppermute x7, waiting for transfers between devices, pairwise_exchange(): part = lax.ppermute(part, axis, [(d, d ^ mask) for d in range(ways)])  34.9 us
    all_to_all x1, waiting for transfers between devices, body(): lax.all_to_all(turned_real, 'gx', split_axis=0, concat_axis=1, tiled=True)  31.5 us
    dot_general x4, matrix products, mat_dot(): jnp.dot(left, right, precision=highest, preferred_element_type=jnp.float32)  19.9 us
    slice x1, local copies, waits for them, and re-layouts, body(): even_rows = paired[:, 0].reshape(half_rows, Q, col_width)  7.69 us
  transfers between devices with their start and end apart: 9, of which 5 were waited for; matrix products, arithmetic and copies ran while one was open for 6% of the time, Pallas kernels for 0%

profile of v1, /device:TPU:0, one launch (start us, length us, event | category | flops | bytes accessed | tf_op | source)
XLA Modules:
  0.0 380.0 jit_solution(12751350019084882052)
XLA Ops:
  0.0 5.3 %copy.14 = f32[2048,512]{0,1:T(8,128)} copy(f32[2048,512]{1,0:T(8,128)} %param.1) | data formatting | bytes 8388608 | tf_op args[0]
  5.3 100.6 %all_to_all.82 = f32[2048,4,128]{0,2,1:T(8,128)} all-to-all(f32[2048,4,128]{0,2,1:T(8,128)} %bitcast.77), channel_id=1, replica_groups=mesh['gx'=8,'gy'=4] {'gy'}, dimensions={1} | all-to-all | bytes 8388608 | tf_op jit(solution)/shard_map/all_to_all | solution.py:45
  105.9 5.3 %copy.15 = f32[4,2048,128]{2,1,0:T(8,128)} copy(f32[4,2048,128]{1,2,0:T(8,128)} %bitcast.75) | data formatting | bytes 8388608 | tf_op jit(solution)/shard_map/all_to_all | solution.py:45
  111.2 7.7 %fusion.96 = (f32[4096,1,128]{2,1,0:T(1,128)}, f32[4096,1,128]{2,1,0:T(1,128)S(1)}) fusion(f32[4096,2,128]{2,1,0:T(2,128)} %bitcast.74), kind=kLoop, calls=%fused_computation.126 | loop fusion | bytes 8388608 | tf_op jit(solution)/shard_map/slice | solution.py:52
  118.9 1.2 copy.16
  120.1 1.5 rev.4
  121.6 4.9 %all-to-all-start.1 = ((f32[16,256,128]{2,0,1:T(8,128)}), f32[16,256,128]{2,0,1:T(8,128)}, u32[]{:S(2)}, u32[]{:S(2)}) async-start(f32[16,256,128]{2,0,1:T(8,128)} %rev.4), calls=%async_computation.1 | async-start | bytes 4194304 | tf_op jit(solution)/shard_map/all_to_all | solution.py:56
  126.5 0.2 broadcast_in_dim.2
  126.8 2.6 constant_dynamic-slice_fusion
  129.4 0.4 collective-permute-start
  129.7 1.6 collective-permute-start.1
  131.4 0.5 fusion.57
  131.9 0.1 collective-permute-start.2
  132.0 1.7 collective-permute-start.3
  133.7 0.1 collective-permute-start.4
  133.8 0.0 collective-permute-done
  133.8 2.6 collective-permute-start.5
  136.4 1.0 constant_dynamic-update-slice_fusion.6
  137.4 20.5 %collective-permute-done.1 = f32[16,32,128]{2,1,0:T(8,128)} collective-permute-done((f32[16,32,128]{2,1,0:T(8,128)}, f32[16,32,128]{2,1,0:T(8,128)}, u32[]{:S(2)}, u32[]{:S(2)}) %collective-permute-start.1) | collective-permute-done | bytes 262176 | tf_op jit(solution)/shard_map/ppermute | solution.py:23
  157.9 0.1 collective-permute-start.6
  157.9 1.0 constant_dynamic-update-slice_fusion.5
  158.9 3.5 collective-permute-done.2
  162.4 1.0 constant_dynamic-update-slice_fusion.4
  163.3 0.0 collective-permute-done.3
  163.4 0.0 collective-permute-done.4
  163.4 6.5 %collective-permute-done.5 = f32[16,32,128]{2,1,0:T(8,128)S(1)} collective-permute-done((f32[16,32,128]{2,1,0:T(8,128)S(1)}, f32[16,32,128]{2,1,0:T(8,128)S(1)}, u32[]{:S(2)}, u32[]{:S(2)}) %collective-permute-start.5) | collective-permute-done | bytes 262176 | tf_op jit(solution)/shard_map/ppermute | solution.py:23
  169.9 4.5 %collective-permute-done.6 = f32[16,32,128]{2,1,0:T(8,128)S(1)} collective-permute-done((f32[16,32,128]{2,1,0:T(8,128)S(1)}, f32[16,32,128]{2,1,0:T(8,128)S(1)}, u32[]{:S(2)}, u32[]{:S(2)}) %collective-permute-start.6) | collective-permute-done | bytes 262176 | tf_op jit(solution)/shard_map/ppermute | solution.py:23
  174.4 0.0 all-to-all-done.1
  174.4 2.2 copy.18
  176.7 5.0 %fusion.7 = f32[256,4096]{1,0:T(8,128)S(1)} fusion(f32[16,8,32,128]{3,2,1,0:T(8,128)S(1)} %bitcast.71, s32[128]{0:T(128)S(1)} %iota_subtract_fusion), kind=kOutput, calls=%fused_computation.14 | convolution fusion | flops 1611071488 | bytes 6291968 | tf_op jit(solution)/shard_map/dot_general | solution.py:29
  181.6 5.0 %fusion.5 = f32[256,4096]{1,0:T(8,128)S(1)} fusion(f32[16,8,32,128]{3,2,1,0:T(8,128)S(1)} %bitcast.72, s32[128]{0:T(128)S(1)} %iota_subtract_fusion), kind=kOutput, calls=%fused_computation.12 | convolution fusion | flops 1611071488 | bytes 6291968 | tf_op jit(solution)/shard_map/dot_general | solution.py:29
  186.6 4.9 %fusion.3 = f32[32,8,32,128]{3,1,2,0:T(8,128)S(1)} fusion(f32[256,4096]{1,0:T(8,128)S(1)} %fusion.7, f32[16,8,32,128]{3,2,1,0:T(8,128)S(1)} %bitcast.69), kind=kOutput, calls=%fused_computation.10 | convolution fusion | flops 1612120064 | bytes 10485760 | tf_op jit(solution)/shard_map/dot_general | solution.py:29
  191.6 0.8 copy.26
  192.3 5.0 %fusion.4 = f32[32,8,32,128]{3,1,2,0:T(8,128)S(1)} fusion(f32[256,4096]{1,0:T(8,128)S(1)} %fusion.5, f32[16,8,32,128]{3,2,1,0:T(8,128)S(1)} %bitcast.70), kind=kOutput, calls=%fused_computation.11 | convolution fusion | flops 1613168640 | bytes 10485760 | tf_op jit(solution)/shard_map/dot_general | solution.py:29
  197.3 0.8 copy.27
  198.1 4.8 %fusion.1 = (f32[256,32,128]{2,1,0:T(8,128)}, f32[256,32,128]{2,1,0:T(8,128)S(1)}) fusion(f32[32,8,32,128]{3,2,1,0:T(8,128)S(1)} %copy.27, f32[32,8,32,128]{3,2,1,0:T(8,128)S(1)} %copy.26, f32[256,32]{1,0:T(8,128)S(1)} %get-tuple-element.20, f32[256,32]{1,0:T(8,128)S(1)} %get-tuple-element.19), kind=kLoop, calls=%fused_computation.5 | loop fusion | flops 6291456 | bytes 16842752 | tf_op jit(solution)/shard_map/add | solution.py:83
  202.9 52.3 %all_to_all.83 = f32[256,32,128]{2,1,0:T(8,128)} all-to-all(f32[256,32,128]{2,1,0:T(8,128)S(1)} %get-tuple-element.6), channel_id=1, replica_groups=mesh['gx'=8,'gy'=4] {'gx'}, dimensions={0} | all-to-all | bytes 8388608 | tf_op jit(solution)/shard_map/all_to_all | solution.py:87
  255.2 4.5 %all-to-all-start.2 = ((f32[256,32,128]{2,1,0:T(8,128)}), f32[256,32,128]{2,1,0:T(8,128)}, u32[]{:S(2)}, u32[]{:S(2)}) async-start(f32[256,32,128]{2,1,0:T(8,128)} %get-tuple-element.5), calls=%async_computation.2 | async-start | bytes 8388608 | tf_op jit(solution)/shard_map/all_to_all | solution.py:86
  259.8 0.1 dynamic_slice.27
  259.8 0.2 fusion.63
  260.0 2.8 copy.20
  262.9 7.1 %fusion.19 = f32[256,32,128]{2,0,1:T(8,128)} fusion(f32[32,256,128]{2,1,0:T(8,128)S(1)} %bitcast.67), kind=kOutput, calls=%fused_computation.29 | convolution fusion | flops 3222142976 | bytes 8388608 | tf_op jit(solution)/shard_map/jb,kbc->jkc/dot_general | solution.py:93
  270.0 7.3 %fusion.21 = f32[256,32,128]{2,0,1:T(8,128)} fusion(f32[32,256,128]{2,1,0:T(8,128)S(1)} %bitcast.68), kind=kOutput, calls=%fused_computation.31 | convolution fusion | flops 3222142976 | bytes 8388608 | tf_op jit(solution)/shard_map/jb,kbc->jkc/dot_general | solution.py:96
  277.3 31.5 %all-to-all-done.2 = f32[256,32,128]{2,1,0:T(8,128)} async-done(((f32[256,32,128]{2,1,0:T(8,128)}), f32[256,32,128]{2,1,0:T(8,128)}, u32[]{:S(2)}, u32[]{:S(2)}) %all-to-all-start.2) | async-done | bytes 4194336 | tf_op jit(solution)/shard_map/all_to_all | solution.py:86
  308.8 2.8 copy.19
  311.7 0.0 copy-start
  311.7 0.0 copy-start.1
  311.7 4.8 %fusion.23 = f32[256,32,128]{2,0,1:T(8,128)S(1)} fusion(f32[32,256,128]{2,1,0:T(8,128)S(1)} %bitcast.65), kind=kOutput, calls=%fused_computation.33 | convolution fusion | flops 3222142976 | bytes 8388608 | tf_op jit(solution)/shard_map/jb,kbc->jkc/dot_general | solution.py:93
  316.4 0.0 copy-done
  316.5 0.0 copy-done.1
  316.5 6.1 %add_multiply_fusion = f32[256,32,128]{2,0,1:T(8,128)S(1)} fusion(f32[256,32,128]{2,0,1:T(8,128)S(1)} %copy-done.1, f32[256,32,128]{2,0,1:T(8,128)S(1)} %fusion.23, f32[256,32,128]{2,0,1:T(8,128)S(1)} %copy-done, f32[32,256,128]{2,1,0:T(8,128)S(1)} %bitcast.66, f32[256,32]{0,1:T(8,128)S(1)} %get-tuple-element.18, f32[256,32]{0,1:T(8,128)S(1)} %get-tuple-element.17), kind=kOutput, calls=%fused_computation.9 | convolution fusion | flops 3228434432 | bytes 21037056 | tf_op jit(solution)/shard_map/jb,kbc->jkc/dot_general | solution.py:96
  322.6 2.7 copy.21
  325.3 51.5 %all_to_all.84 = f32[256,32,128]{2,1,0:T(8,128)S(1)} all-to-all(f32[256,32,128]{2,1,0:T(8,128)S(1)} %copy.21), channel_id=1, replica_groups=mesh['gx'=8,'gy'=4] {'gx'}, dimensions={0} | all-to-all | bytes 8388608 | tf_op jit(solution)/shard_map/all_to_all | solution.py:102
  376.8 2.7 copy.22
  (8 shorter events, 0.1 us)
Async XLA Ops:
  121.6 52.8 %all-to-all-start.1 = ((f32[16,256,128]{2,0,1:T(8,128)}), f32[16,256,128]{2,0,1:T(8,128)}, u32[]{:S(2)}, u32[]{:S(2)}) async-start(f32[16,256,128]{2,0,1:T(8,128)} %rev.4), calls=%async_computation.1 | async-start | bytes 4194304 | tf_op jit(solution)/shard_map/all_to_all | solution.py:56
  129.4 4.5 %collective-permute-start = (f32[16,32,128]{2,1,0:T(8,128)}, f32[16,32,128]{2,1,0:T(8,128)}, u32[]{:S(2)}, u32[]{:S(2)}) collective-permute-start(f32[16,32,128]{2,1,0:T(8,128)} %get-tuple-element.15), channel_id=1, source_target_pairs={{0,4},{4,0},{8,12},{12,8},{16,20},{20,16},{24,28},{28,24},{1,5},{5... | collective-permute-start | bytes 786440 | tf_op jit(solution)/shard_map/ppermute | solution.py:23
  129.7 28.1 %collective-permute-start.1 = (f32[16,32,128]{2,1,0:T(8,128)}, f32[16,32,128]{2,1,0:T(8,128)}, u32[]{:S(2)}, u32[]{:S(2)}) collective-permute-start(f32[16,32,128]{2,1,0:T(8,128)} %get-tuple-element.14), channel_id=1, source_target_pairs={{0,8},{4,12},{8,0},{12,4},{16,24},{20,28},{24,16},{28,20},{1,9},{5... | collective-permute-start | bytes 786440 | tf_op jit(solution)/shard_map/ppermute | solution.py:23
  131.9 30.4 %collective-permute-start.2 = (f32[16,32,128]{2,1,0:T(8,128)}, f32[16,32,128]{2,1,0:T(8,128)}, u32[]{:S(2)}, u32[]{:S(2)}) collective-permute-start(f32[16,32,128]{2,1,0:T(8,128)} %get-tuple-element.13), channel_id=1, source_target_pairs={{0,12},{4,8},{8,4},{12,0},{16,28},{20,24},{24,20},{28,16},{1,13},{... | collective-permute-start | bytes 786440 | tf_op jit(solution)/shard_map/ppermute | solution.py:23
  132.0 31.3 %collective-permute-start.3 = (f32[16,32,128]{2,1,0:T(8,128)S(1)}, f32[16,32,128]{2,1,0:T(8,128)S(1)}, u32[]{:S(2)}, u32[]{:S(2)}) collective-permute-start(f32[16,32,128]{2,1,0:T(8,128)S(1)} %get-tuple-element.12), channel_id=1, source_target_pairs={{0,16},{4,20},{8,24},{12,28},{16,0},{20,4},{24,8},{28,12},{1,17},{... | collective-permute-start | bytes 786440 | tf_op jit(solution)/shard_map/ppermute | solution.py:23
  133.7 29.6 %collective-permute-start.4 = (f32[16,32,128]{2,1,0:T(8,128)S(1)}, f32[16,32,128]{2,1,0:T(8,128)S(1)}, u32[]{:S(2)}, u32[]{:S(2)}) collective-permute-start(f32[16,32,128]{2,1,0:T(8,128)S(1)} %get-tuple-element.11), channel_id=1, source_target_pairs={{0,20},{4,16},{8,28},{12,24},{16,4},{20,0},{24,12},{28,8},{1,21},{... | collective-permute-start | bytes 786440 | tf_op jit(solution)/shard_map/ppermute | solution.py:23
  133.8 36.1 %collective-permute-start.5 = (f32[16,32,128]{2,1,0:T(8,128)S(1)}, f32[16,32,128]{2,1,0:T(8,128)S(1)}, u32[]{:S(2)}, u32[]{:S(2)}) collective-permute-start(f32[16,32,128]{2,1,0:T(8,128)S(1)} %get-tuple-element.10), channel_id=1, source_target_pairs={{0,24},{4,28},{8,16},{12,20},{16,8},{20,12},{24,0},{28,4},{1,25},{... | collective-permute-start | bytes 786440 | tf_op jit(solution)/shard_map/ppermute | solution.py:23
  157.9 16.5 %collective-permute-start.6 = (f32[16,32,128]{2,1,0:T(8,128)S(1)}, f32[16,32,128]{2,1,0:T(8,128)S(1)}, u32[]{:S(2)}, u32[]{:S(2)}) collective-permute-start(f32[16,32,128]{2,1,0:T(8,128)S(1)} %get-tuple-element.9), channel_id=1, source_target_pairs={{0,28},{4,24},{8,20},{12,16},{16,12},{20,8},{24,4},{28,0},{1,29},{... | collective-permute-start | bytes 786440 | tf_op jit(solution)/shard_map/ppermute | solution.py:23
  255.2 53.7 %all-to-all-start.2 = ((f32[256,32,128]{2,1,0:T(8,128)}), f32[256,32,128]{2,1,0:T(8,128)}, u32[]{:S(2)}, u32[]{:S(2)}) async-start(f32[256,32,128]{2,1,0:T(8,128)} %get-tuple-element.5), calls=%async_computation.2 | async-start | bytes 8388608 | tf_op jit(solution)/shard_map/all_to_all | solution.py:86
  311.7 4.8 %copy-start = (f32[256,32,128]{2,0,1:T(8,128)S(1)}, f32[256,32,128]{2,0,1:T(8,128)}, u32[]{:S(2)}) copy-start(f32[256,32,128]{2,0,1:T(8,128)} %fusion.19) | copy-start | bytes 12582916
  311.7 4.8 %copy-start.1 = (f32[256,32,128]{2,0,1:T(8,128)S(1)}, f32[256,32,128]{2,0,1:T(8,128)}, u32[]{:S(2)}) copy-start(f32[256,32,128]{2,0,1:T(8,128)} %fusion.21) | copy-start | bytes 12582916
